TPU v7x, 32 devices: a whole 2x2x4 slice. The times are simulated.
32 devices in a mesh: basin: 2 (over x), recv: 8 (over z, y), src: 2 (over core).
Axes of the slice: x: 2, y: 2, z: 4, core: 2. Of those that a mesh axis runs over, the one named last changes fastest.
Arguments:
- positions: float32 [3, 4096], P(None, ('basin', 'recv', 'src')), parts along dimension 1, may hold values from -1.1 to 1.1, as said below
- normals: float32 [3, 4096], P(None, ('basin', 'recv', 'src')), parts along dimension 1, may hold values from -1 to 1, as said below
- area: float32 [4096], P(('basin', 'recv', 'src')), parts along dimension 0, may hold values from 0.0009765625 to 0.0078125
- albedo: float32 [4096], P(('basin', 'recv', 'src')), parts along dimension 0, may hold values from 0.1 to 0.6
- conductivity: float32 [4096], P(('basin', 'recv', 'src')), parts along dimension 0, may hold values from 0.05 to 0.4
- soil: float32 [32, 4096], P(None, ('basin', 'recv', 'src')), parts along dimension 1, may hold values from 0.5 to 1.2
- sun_tan: float32 [16], replicated, may hold values from 0.05 to 2
- samples: int32 [32, 32], P(('basin', 'recv', 'src')), parts along dimension 0, may hold values from 1 to 2047
- occupancy: int32 [32, 16], P('basin'), parts along dimension 0, may hold values 0 or 1
Outputs:
- soil_final: float32 [32, 4096], P(None, ('basin', 'recv', 'src')), parts along dimension 1
- bounce: float32 [16, 4096], P(None, ('basin', 'recv', 'src')), parts along dimension 1
There are 2 independent parts, one for each index of `basin`. A program takes and returns all parts, laid end to end along the dimension named above; an argument that names none is the same for every part. Nothing has to cross between parts.
Inputs may be any that keep to these rules, and one draw needn't show every extreme that they name: `positions`: facets lie on a bowl below z = 0. `normals`: each column has unit length.
All inputs are finite; a program needn't handle non-finite values.
Results may differ from a plain program's by a relative error of at most 0.0003.
Values may be sent and summed in bfloat16 or wider, within the bound.
A program may use at most 64 MiB of HBM per device.

v0:
```python
import functools
import math

import jax
import jax.numpy as jnp
from jax import lax
from jax.experimental import pallas as pl
from jax.experimental.pallas import tpu as pltpu
from jax.sharding import PartitionSpec as P

solar_flux = 2.0
emissivity = 0.9
surface_gain = 0.1
shade_width = 0.1
reach_offset = 0.05
GROUP = 8
CHUNK = 16


def fourth(value):
    square = value * value
    return square * square


def column(row, count):
    wide = jnp.broadcast_to(row[:, :count], (count, count))
    here = lax.broadcasted_iota(jnp.int32, (count, count), 0) == lax.broadcasted_iota(
        jnp.int32, (count, count), 1
    )
    return jnp.sum(jnp.where(here, wide, 0.0), axis=1, keepdims=True)


def kernel(
    n_recv,
    n_src,
    pos_in,
    nrm_in,
    area_in,
    alb_in,
    cond_in,
    soil_in,
    tan_in,
    smp_in,
    occ_in,
    bounce_ref,
    heat_ref,
    cond_ref,
    soil_ref,
    pos_ref,
    nrm_ref,
    area_ref,
    alb_ref,
    tan_ref,
    smp_ref,
    occ_ref,
    near,
    far,
    planes,
    shifts,
    cols,
    view,
    direct_ref,
    lit_ref,
    tall_tan,
    radg,
    sems,
    loads,
):
    n = n_recv * n_src
    width = pos_ref.shape[1]
    n_samples = smp_ref.shape[1]
    epochs = tan_ref.shape[1]
    bits = width.bit_length() - 1
    few = n <= 16
    me = lax.axis_index("recv") * n_src + lax.axis_index("src")

    def peer(k):
        p = (me + (n - k)) & (n - 1)
        return {"recv": p >> (n_src.bit_length() - 1), "src": p & (n_src - 1)}

    def over(first, last, step):
        if few:
            for k in sorted(range(first, last), key=lambda k: abs(2 * k - n)):
                step(k)
        else:
            lax.fori_loop(first, last, lambda k, c: (step(k), c)[1], 0)

    barrier = pltpu.get_barrier_semaphore()
    over(
        1,
        n,
        lambda k: pl.semaphore_signal(
            barrier, inc=1, device_id=peer(k), device_id_type=pl.DeviceIdType.MESH
        ),
    )
    pairs = (
        (pos_in, pos_ref),
        (smp_in, smp_ref),
        (nrm_in, nrm_ref),
        (area_in, area_ref),
        (tan_in, tan_ref),
        (soil_in, soil_ref),
        (alb_in, alb_ref),
        (cond_in, cond_ref),
        (occ_in.at[pl.ds(me, 1)], occ_ref),
    )
    fetched = [
        pltpu.make_async_copy(there, here, loads.at[i]) for i, (there, here) in enumerate(pairs)
    ]
    for copy in fetched:
        copy.start()
    for copy in fetched[:4]:
        copy.wait()
    near[0, 0:3, :] = pos_ref[...]
    near[0, 3:4, 0:n_samples] = smp_ref[...].astype(jnp.float32)
    far[0, 0:3, :] = nrm_ref[...]
    far[0, 3:4, :] = area_ref[...]
    for copy in fetched[4:]:
        copy.wait()
    pl.semaphore_wait(barrier, n - 1)

    def send(ref, k, which):
        pltpu.make_async_remote_copy(
            src_ref=ref.at[0],
            dst_ref=ref.at[k],
            send_sem=sems.at[which],
            recv_sem=sems.at[which + 1],
            device_id=peer(k),
            device_id_type=pl.DeviceIdType.MESH,
        ).start()

    def everyone(ref, which):
        return pltpu.make_async_remote_copy(
            src_ref=ref.at[pl.ds(1, n - 1)],
            dst_ref=ref.at[pl.ds(1, n - 1)],
            send_sem=sems.at[which],
            recv_sem=sems.at[which + 1],
            device_id=peer(1),
            device_id_type=pl.DeviceIdType.MESH,
        )

    over(1, n, lambda k: send(near, k, 0))
    over(1, n, lambda k: send(far, k, 4))

    mine = near[0]
    tall = jnp.transpose(jnp.concatenate([mine, far[0]], axis=0))
    for c, at in enumerate((0, 1, 2, 4, 5, 6)):
        cols[c] = jnp.broadcast_to(tall[:, at : at + 1], (width, width))
    tan = column(tan_ref[...], epochs)
    angle = (
        2.0
        * math.pi
        * lax.broadcasted_iota(jnp.int32, (epochs, width), 0).astype(jnp.float32)
        / epochs
    )
    cos_e = 1.0 / jnp.sqrt(1.0 + tan * tan)
    incidence = (
        cos_e * jnp.cos(angle) * nrm_ref[0:1, :]
        + cos_e * jnp.sin(angle) * nrm_ref[1:2, :]
        + tan * cos_e * nrm_ref[2:3, :]
    )
    lit_ref[...] = solar_flux * jnp.maximum(incidence, 0.0)
    tall_tan[...] = jnp.broadcast_to(tan, (epochs, width))
    infrared = emissivity * fourth(soil_ref[0:1, :])

    everyone(near, 0).wait_recv()
    for c in range(3):
        planes[c] = near[:, c, :]
    rows = near[:, 3, :]
    shifts[0:n, :] = rows
    shifts[n : 2 * n, :] = rows

    lane = lax.broadcasted_iota(jnp.int32, (GROUP, width), 1)
    px, py, pz = (jnp.broadcast_to(mine[c : c + 1, :], (GROUP, width)) for c in range(3))

    def azimuths(group):
        offset = n - me + group * GROUP
        steps = shifts[pl.ds(offset, GROUP), :].astype(jnp.int32)
        best = jnp.full((GROUP, width), -1e30, jnp.float32)
        for s in range(n_samples):
            shift = jnp.broadcast_to(steps[:, s : s + 1], (GROUP, width))
            row = ((shift + (width - 1) - lane) >> bits) & (n - 1)
            within = row & (GROUP - 1)
            part = row >> (GROUP.bit_length() - 1)
            turn = (lane + shift) & (width - 1)
            found = []
            for c in range(3):
                picked = None
                for g in range(n // GROUP):
                    block = planes[c, g * GROUP : (g + 1) * GROUP, :]
                    got = jnp.take_along_axis(block, within, axis=0)
                    picked = got if picked is None else jnp.where(part == g, got, picked)
                found.append(jnp.take_along_axis(picked, turn, axis=1))
            dx = found[0] - px
            dy = found[1] - py
            reach = jnp.sqrt(dx * dx + dy * dy) + reach_offset
            best = jnp.maximum(best, (found[2] - pz) / reach)
        start = group * GROUP
        here = pl.ds(start if few else pl.multiple_of(start, GROUP), GROUP)
        direct = lit_ref[here, :] * jax.nn.sigmoid((tall_tan[here, :] - best) / shade_width)
        direct_ref[here, :] = direct
        radg[0, group] = (alb_ref[...] * direct + infrared).astype(jnp.bfloat16)
        over(1, n, lambda k: send(radg.at[:, group], k, 2))

    over(0, n // GROUP, azimuths)

    def see(k, carry):
        weight = occ_ref[0, lax.rem(me + k, n)].astype(jnp.float32)
        sx, sy, sz = (near[k, c : c + 1, :] for c in range(3))
        ox, oy, oz, size = (far[k, c : c + 1, :] for c in range(4))
        scale = size * weight / math.pi
        for i in range(width // CHUNK):
            at = slice(i * CHUNK, (i + 1) * CHUNK)
            dx = sx - cols[0, at, :]
            dy = sy - cols[1, at, :]
            dz = sz - cols[2, at, :]
            facing = cols[3, at, :] * dx + cols[4, at, :] * dy + cols[5, at, :] * dz
            toward = -(ox * dx + oy * dy + oz * dz)
            spread = dx * dx + dy * dy + dz * dz + size
            seen = jnp.maximum(facing, 0.0) * jnp.maximum(toward, 0.0) * scale
            view[k, at, :] = (seen / (spread * spread)).astype(jnp.bfloat16)
        return carry

    everyone(far, 4).wait_recv()
    lax.fori_loop(0, n, see, 0)
    everyone(radg, 2).wait_recv()

    def fold(k, total):
        sent = jnp.concatenate([radg[k, g] for g in range(epochs // GROUP)], axis=0)
        return total + lax.dot_general(
            sent, view[k], (((1,), (1,)), ((), ())), preferred_element_type=jnp.float32
        )

    total = jnp.zeros((epochs, width), jnp.float32)
    if few:
        for k in range(n):
            total = fold(k, total)
    else:
        total = lax.fori_loop(0, n, fold, total)
    bounce_ref[...] = total
    keep = surface_gain * (1.0 - alb_ref[...])
    heat_ref[...] = keep * (direct_ref[...] + total)
    everyone(near, 0).wait_send()
    everyone(far, 4).wait_send()
    everyone(radg, 2).wait_send()


def conduct(bounce_in, heat_ref, cond_ref, soil_ref, final_ref, bounce_ref):
    layers, width = soil_ref.shape
    epochs = heat_ref.shape[0]
    bounce_ref[...] = bounce_in[...]
    cond = cond_ref[...]
    first = lax.broadcasted_iota(jnp.int32, (layers, width), 0) == 0
    last = lax.broadcasted_iota(jnp.int32, (layers, width), 0) == layers - 1

    def advance(t, temps):
        below = jnp.where(last, temps, pltpu.roll(temps, layers - 1, 0))
        above = jnp.where(first, temps, pltpu.roll(temps, 1, 0))
        temps = temps + cond * ((below - temps) - (temps - above))
        gain = heat_ref[pl.ds(t, 1), :] - (surface_gain * emissivity) * fourth(temps)
        return jnp.where(first, temps + gain, temps)

    temps = soil_ref[...]
    if epochs <= 16:
        for t in range(epochs):
            temps = advance(t, temps)
    else:
        temps = lax.fori_loop(0, epochs, advance, temps)
    final_ref[...] = temps


def body(positions, normals, area, albedo, conductivity, soil, sun_tan, samples, occupancy):
    n_recv = lax.axis_size("recv")
    n_src = lax.axis_size("src")
    n = n_recv * n_src
    width = positions.shape[1]
    epochs = sun_tan.shape[0]
    vmem = pl.BlockSpec(memory_space=pltpu.VMEM)
    f32 = jnp.float32
    n_samples = samples.shape[1]
    held = pl.pallas_call(
        functools.partial(kernel, n_recv, n_src),
        out_shape=(
            pltpu.VMEM((epochs, width), f32),
            pltpu.VMEM((epochs, width), f32),
            pltpu.VMEM((1, width), f32),
            pltpu.VMEM(soil.shape, f32),
        ),
        in_specs=[pl.BlockSpec(memory_space=pl.ANY)] * 9,
        out_specs=(vmem,) * 4,
        scratch_shapes=[
            pltpu.VMEM((3, width), f32),
            pltpu.VMEM((3, width), f32),
            pltpu.VMEM((1, width), f32),
            pltpu.VMEM((1, width), f32),
            pltpu.VMEM((1, epochs), f32),
            pltpu.VMEM((1, n_samples), jnp.int32),
            pltpu.SMEM((1, occupancy.shape[1]), jnp.int32),
            pltpu.VMEM((n, 4, width), f32),
            pltpu.VMEM((n, 4, width), f32),
            pltpu.VMEM((3, n, width), f32),
            pltpu.VMEM((2 * n, width), f32),
            pltpu.VMEM((6, width, width), f32),
            pltpu.VMEM((n, width, width), jnp.bfloat16),
            pltpu.VMEM((epochs, width), f32),
            pltpu.VMEM((epochs, width), f32),
            pltpu.VMEM((epochs, width), f32),
            pltpu.VMEM((n, epochs // GROUP, GROUP, width), jnp.bfloat16),
            pltpu.SemaphoreType.DMA((6,)),
            pltpu.SemaphoreType.DMA((9,)),
        ],
        compiler_params=pltpu.CompilerParams(collective_id=0, has_side_effects=True),
    )(
        positions,
        normals,
        area.reshape(1, width),
        albedo.reshape(1, width),
        conductivity.reshape(1, width),
        soil,
        sun_tan.reshape(1, epochs),
        samples,
        occupancy,
    )
    return pl.pallas_call(
        conduct,
        out_shape=(
            jax.ShapeDtypeStruct(soil.shape, f32),
            jax.ShapeDtypeStruct((epochs, width), f32),
        ),
        in_specs=[vmem] * 4,
        out_specs=(vmem, vmem),
    )(*(pltpu.with_memory_space_constraint(value, pltpu.VMEM) for value in held))


def solution(mesh):
    in_specs = (
        P(None, ("basin", "recv", "src")),
        P(None, ("basin", "recv", "src")),
        P(("basin", "recv", "src")),
        P(("basin", "recv", "src")),
        P(("basin", "recv", "src")),
        P(None, ("basin", "recv", "src")),
        P(),
        P(("basin", "recv", "src"), None),
        P("basin", None),
    )
    out_specs = (P(None, ("basin", "recv", "src")), P(None, ("basin", "recv", "src")))
    return jax.shard_map(body, mesh=mesh, in_specs=in_specs, out_specs=out_specs, check_vma=False)
```

profile of v0, /device:TPU:0, one launch (start us, length us, event | category | flops | bytes accessed | tf_op | source)
XLA Modules:
  0.0 17.4 jit_solution(3611295210618017264)
XLA Ops:
  0.6 15.9 %shard_map.104 = (f32[16,128]{1,0:T(8,128)S(1)}, f32[16,128]{1,0:T(8,128)S(1)}, f32[1,128]{1,0:T(1,128)S(1)}, f32[32,128]{1,0:T(8,128)S(1)}) custom-call(f32[3,128]{1,0:T(4,128)} %pos_in.1, f32[3,128]{1,0:T(4,128)} %nrm_in.1, f32[1,128]{1,0:T(1,128)} %bitcast.4, f32[1,128]{1,0:T(1,128)} %bitcast.5, f32[1,128]{1,0:T(1,128)} %bitcast.6, f32[32,128]{1,0:T(8,128)} %soil_in.1, ...), custom_call_target="tpu_custom_call" | custom-call | tf_op jit(solution)/shard_map/pallas_call | solution.py:281
  16.6 0.8 %shard_map.105 = (f32[32,128]{1,0:T(8,128)}, f32[16,128]{1,0:T(8,128)}) custom-call(f32[16,128]{1,0:T(8,128)S(1)} %get-tuple-element.6.bounce_in, f32[16,128]{1,0:T(8,128)S(1)} %get-tuple-element.7.heat_ref, f32[1,128]{1,0:T(1,128)S(1)} %get-tuple-element.8.cond_ref, f32[32,128]{1,0:T(8,128)S(1)} %get-tuple-element.9.soil_ref), custom_call_target="tpu_custom_call" | custom-call | tf_op jit(solution)/shard_map/pallas_call | solution.py:324
where the time goes:
time: 17.6 us; the launch traced here: 17.4 us
  Pallas kernels  16.7 us (95%)
  between operations  0.64 us (4%)
    pallas_call x1, Pallas kernels, body(): pl.pallas_call(functools.partial(kernel, n_recv, n_src), out_shape=(pltpu...  15.9 us
    pallas_call x1, Pallas kernels, body(): pl.pallas_call(conduct, out_shape=(jax.ShapeDtypeStruct(soil.shape, f32),...  0.81 us

commit v1 on v0

--- a/solution.py
+++ b/solution.py
@@ -15,6 +15,7 @@
 reach_offset = 0.05
 GROUP = 8
 CHUNK = 16
+TURNS = 32
 
 
 def fourth(value):
@@ -245,6 +246,228 @@
     everyone(radg, 2).wait_send()
 
 
+def step(
+    n_recv,
+    n_src,
+    pos_in,
+    nrm_in,
+    area_in,
+    alb_in,
+    cond_in,
+    soil_in,
+    tan_in,
+    smp_in,
+    occ_in,
+    bounce_ref,
+    heat_ref,
+    cond_ref,
+    soil_ref,
+    alb_ref,
+    tan_ref,
+    occ_ref,
+    near,
+    far,
+    smp,
+    planes,
+    table,
+    cols,
+    view,
+    sun_ref,
+    direct_ref,
+    lit_ref,
+    hello,
+    sent,
+    got,
+    loads,
+):
+    n = n_recv * n_src
+    width = alb_ref.shape[1]
+    n_samples = smp.shape[2]
+    epochs = tan_ref.shape[1]
+    bits = width.bit_length() - 1
+    rows = 2 * n
+    me = lax.axis_index("recv") * n_src + lax.axis_index("src")
+
+    def device(p):
+        return {"recv": p >> (n_src.bit_length() - 1), "src": p & (n_src - 1)}
+
+    def greet(sem, p):
+        pl.semaphore_signal(sem, inc=1, device_id=device(p), device_id_type=pl.DeviceIdType.MESH)
+
+    def each(first, last, do):
+        lax.fori_loop(first, last, lambda p, c: (do(p), c)[1], 0)
+
+    own = pl.ds(me, 1)
+    pairs = [(pos_in.at[pl.ds(c, 1)], near.at[c, own]) for c in range(3)]
+    pairs += [(smp_in, smp.at[me])]
+    pairs += [(nrm_in.at[pl.ds(c, 1)], far.at[c, own]) for c in range(3)]
+    pairs += [(area_in, far.at[3, own]), (alb_in, far.at[4, own]), (soil_in.at[pl.ds(0, 1)], far.at[5, own])]
+    pairs += [
+        (alb_in, alb_ref),
+        (tan_in, tan_ref),
+        (soil_in, soil_ref),
+        (cond_in, cond_ref),
+        (occ_in.at[own], occ_ref),
+    ]
+    fetched = [
+        pltpu.make_async_copy(there, here, loads.at[i]) for i, (there, here) in enumerate(pairs)
+    ]
+    for copy in fetched:
+        copy.start()
+    barrier = pltpu.get_barrier_semaphore()
+    each(me + 1, n, lambda p: greet(barrier, p))
+    pl.when(me > 0)(lambda: pl.semaphore_wait(barrier, me))
+    each(0, me, lambda p: greet(hello.at[me], p))
+
+    def parts(p, which):
+        ref = (near, smp, far)[which]
+        return ref.at[p] if which == 1 else ref.at[:, pl.ds(p, 1)]
+
+    def remote(slot, to, which):
+        return pltpu.make_async_remote_copy(
+            src_ref=parts(slot, which),
+            dst_ref=parts(slot, which),
+            send_sem=sent.at[which],
+            recv_sem=got.at[which, slot],
+            device_id=device(to),
+            device_id_type=pl.DeviceIdType.MESH,
+        )
+
+    for copy in fetched[:4]:
+        copy.wait()
+
+    def first(p):
+        remote(me, p, 0).start()
+        remote(me, p, 1).start()
+
+    each(0, me, first)
+    for copy in fetched[4:10]:
+        copy.wait()
+    each(0, me, lambda p: remote(me, p, 2).start())
+    for copy in fetched[10:]:
+        copy.wait()
+
+    mine = jnp.concatenate([near[:, me, :], far[0:3, me, :]], axis=0)
+    mine = jnp.concatenate([mine, mine[0:2]], axis=0)
+    tall = jnp.transpose(mine)
+    for c in range(6):
+        cols[c] = jnp.broadcast_to(tall[:, c : c + 1], (width, width))
+    tan = column(tan_ref[...], epochs)
+    angle = (
+        2.0
+        * math.pi
+        * lax.broadcasted_iota(jnp.int32, (epochs, width), 0).astype(jnp.float32)
+        / epochs
+    )
+    cos_e = 1.0 / jnp.sqrt(1.0 + tan * tan)
+    sun_ref[0] = cos_e * jnp.cos(angle)
+    sun_ref[1] = cos_e * jnp.sin(angle)
+    sun_ref[2] = jnp.broadcast_to(tan * cos_e, (epochs, width))
+    sun_ref[3] = jnp.broadcast_to(tan, (epochs, width))
+
+    def answer(p):
+        pl.semaphore_wait(hello.at[p], 1)
+        remote(me, p, 0).start()
+        remote(me, p, 1).start()
+        remote(me, p, 2).start()
+
+    each(me + 1, n, answer)
+
+    def see(p):
+        weight = occ_ref[0, p].astype(jnp.float32)
+        row = pl.ds(p, 1)
+        sx, sy, sz = (near[c, row, :] for c in range(3))
+        ox, oy, oz, size = (far[c, row, :] for c in range(4))
+        scale = size * weight / math.pi
+        for i in range(width // CHUNK):
+            at = slice(i * CHUNK, (i + 1) * CHUNK)
+            dx = sx - cols[0, at, :]
+            dy = sy - cols[1, at, :]
+            dz = sz - cols[2, at, :]
+            facing = cols[3, at, :] * dx + cols[4, at, :] * dy + cols[5, at, :] * dz
+            toward = -(ox * dx + oy * dy + oz * dz)
+            spread = dx * dx + dy * dy + dz * dz + size
+            seen = jnp.maximum(facing, 0.0) * jnp.maximum(toward, 0.0) * scale
+            view[p, at, :] = (seen / (spread * spread)).astype(jnp.bfloat16)
+
+    early = n - n // 8
+
+    def arrive(m):
+        p = me ^ m
+        for which in range(3):
+            remote(p, p, which).wait_recv()
+        see(p)
+
+    see(me)
+    each(1, early, arrive)
+    each(early, n, lambda m: [remote(me ^ m, me ^ m, which).wait_recv() for which in range(2)] and None)
+
+    for c in range(3):
+        planes[c, 0:n, :] = near[c]
+        planes[c, n : n + 8, :] = near[c, 0:8]
+    lane = lax.broadcasted_iota(jnp.int32, (8, width), 1)
+
+    def spin(i, carry):
+        for j in range(TURNS):
+            r = i * TURNS + j
+            whole = lane >= r
+            back = (width - r) & (width - 1)
+            for c in range(3):
+                for g in range(n // 8):
+                    here = planes[c, g * 8 : g * 8 + 8, :]
+                    after = planes[c, g * 8 + 1 : g * 8 + 9, :]
+                    turned = pltpu.roll(jnp.where(whole, here, after), back, 1)
+                    table[c, pl.ds(r * rows + g * 8, 8), :] = turned
+                    table[c, pl.ds(r * rows + n + g * 8, 8), :] = turned
+        return carry
+
+    lax.fori_loop(0, width // TURNS, spin, 0)
+
+    def horizons(a, carry):
+        here = [[planes[c, g * 8 : g * 8 + 8, :] for g in range(n // 8)] for c in range(3)]
+        best = [jnp.full((8, width), -1e30, jnp.float32) for g in range(n // 8)]
+        for s in range(n_samples):
+            shift = smp[a, 0, s]
+            start = (shift & (width - 1)) * rows + (shift >> bits)
+            for g in range(n // 8):
+                fx, fy, fz = (table[c, pl.ds(start + g * 8, 8), :] for c in range(3))
+                dx = fx - here[0][g]
+                dy = fy - here[1][g]
+                square = jnp.maximum(dx * dx + dy * dy, 1e-30)
+                reach = square * lax.rsqrt(square) + reach_offset
+                best[g] = jnp.maximum(best[g], (fz - here[2][g]) / reach)
+        line = pl.ds(a, 1)
+        cx, cy, cz, tans = (sun_ref[c, line, :] for c in range(4))
+        for g in range(n // 8):
+            at = slice(g * 8, g * 8 + 8)
+            incidence = cx * far[0, at, :] + cy * far[1, at, :] + cz * far[2, at, :]
+            shade = jax.nn.sigmoid((tans - best[g]) / shade_width)
+            direct = solar_flux * jnp.maximum(incidence, 0.0) * shade
+            direct_ref[a, at, :] = direct
+            lit_ref[a, at, :] = far[4, at, :] * direct + emissivity * fourth(far[5, at, :])
+        return carry
+
+    def last(m):
+        remote(me ^ m, me ^ m, 2).wait_recv()
+        see(me ^ m)
+
+    each(early, n, last)
+    lax.fori_loop(0, epochs, horizons, 0)
+
+    total = jnp.zeros((epochs, width), jnp.float32)
+    for p in range(n):
+        total = total + lax.dot_general(
+            lit_ref[:, p, :].astype(jnp.bfloat16),
+            view[p],
+            (((1,), (1,)), ((), ())),
+            preferred_element_type=jnp.float32,
+        )
+    bounce_ref[...] = total
+    keep = surface_gain * (1.0 - alb_ref[...])
+    heat_ref[...] = keep * (direct_ref[:, me, :] + total)
+    each(1, n, lambda m: [remote(me, me, which).wait_send() for which in range(3)] and None)
+
+
 def conduct(bounce_in, heat_ref, cond_ref, soil_ref, final_ref, bounce_ref):
     layers, width = soil_ref.shape
     epochs = heat_ref.shape[0]
@@ -278,17 +501,30 @@
     vmem = pl.BlockSpec(memory_space=pltpu.VMEM)
     f32 = jnp.float32
     n_samples = samples.shape[1]
-    held = pl.pallas_call(
-        functools.partial(kernel, n_recv, n_src),
-        out_shape=(
-            pltpu.VMEM((epochs, width), f32),
-            pltpu.VMEM((epochs, width), f32),
+    if n <= 16:
+        program = step
+        scratch = [
             pltpu.VMEM((1, width), f32),
-            pltpu.VMEM(soil.shape, f32),
-        ),
-        in_specs=[pl.BlockSpec(memory_space=pl.ANY)] * 9,
-        out_specs=(vmem,) * 4,
-        scratch_shapes=[
+            pltpu.VMEM((1, epochs), f32),
+            pltpu.SMEM((1, occupancy.shape[1]), jnp.int32),
+            pltpu.VMEM((3, n, width), f32),
+            pltpu.VMEM((6, n, width), f32),
+            pltpu.SMEM((n, 1, n_samples), jnp.int32),
+            pltpu.VMEM((3, n + 8, width), f32),
+            pltpu.VMEM((3, width * 2 * n, width), f32),
+            pltpu.VMEM((6, width, width), f32),
+            pltpu.VMEM((n, width, width), jnp.bfloat16),
+            pltpu.VMEM((4, epochs, width), f32),
+            pltpu.VMEM((epochs, n, width), f32),
+            pltpu.VMEM((epochs, n, width), f32),
+            pltpu.SemaphoreType.REGULAR((n,)),
+            pltpu.SemaphoreType.DMA((3,)),
+            pltpu.SemaphoreType.DMA((3, n)),
+            pltpu.SemaphoreType.DMA((15,)),
+        ]
+    else:
+        program = kernel
+        scratch = [
             pltpu.VMEM((3, width), f32),
             pltpu.VMEM((3, width), f32),
             pltpu.VMEM((1, width), f32),
@@ -308,7 +544,18 @@
             pltpu.VMEM((n, epochs // GROUP, GROUP, width), jnp.bfloat16),
             pltpu.SemaphoreType.DMA((6,)),
             pltpu.SemaphoreType.DMA((9,)),
-        ],
+        ]
+    held = pl.pallas_call(
+        functools.partial(program, n_recv, n_src),
+        out_shape=(
+            pltpu.VMEM((epochs, width), f32),
+            pltpu.VMEM((epochs, width), f32),
+            pltpu.VMEM((1, width), f32),
+            pltpu.VMEM(soil.shape, f32),
+        ),
+        in_specs=[pl.BlockSpec(memory_space=pl.ANY)] * 9,
+        out_specs=(vmem,) * 4,
+        scratch_shapes=scratch,
         compiler_params=pltpu.CompilerParams(collective_id=0, has_side_effects=True),
     )(
         positions,

time: 17.6 us -> 15.3 us (0.87)
  Pallas kernels: 16.7 us -> 14.5 us
    pallas_call x1, Pallas kernels: 15.9 us -> 13.6 us  [body(): pl.pallas_call(functools.partial(program, n_recv, n_src), out_shape=(pltp...]
where the time goes in v1:
time: 15.3 us; the launch traced here: 15.1 us
  Pallas kernels  14.5 us (95%)
  between operations  0.64 us (4%)
    pallas_call x1, Pallas kernels, body(): pl.pallas_call(functools.partial(program, n_recv, n_src), out_shape=(pltp...  13.6 us
    pallas_call x1, Pallas kernels, body(): pl.pallas_call(conduct, out_shape=(jax.ShapeDtypeStruct(soil.shape, f32),...  0.81 us

profile of v1, /device:TPU:0, one launch (start us, length us, event | category | flops | bytes accessed | tf_op | source)
XLA Modules:
  0.0 15.1 jit_solution(10379042567865123629)
XLA Ops:
  0.6 13.6 %shard_map.104 = (f32[16,128]{1,0:T(8,128)S(1)}, f32[16,128]{1,0:T(8,128)S(1)}, f32[1,128]{1,0:T(1,128)S(1)}, f32[32,128]{1,0:T(8,128)S(1)}) custom-call(f32[3,128]{1,0:T(4,128)} %pos_in.1, f32[3,128]{1,0:T(4,128)} %nrm_in.1, f32[1,128]{1,0:T(1,128)} %bitcast.4, f32[1,128]{1,0:T(1,128)} %bitcast.5, f32[1,128]{1,0:T(1,128)} %bitcast.6, f32[32,128]{1,0:T(8,128)} %soil_in.1, ...), custom_call_target="tpu_custom_call" | custom-call | tf_op jit(solution)/shard_map/pallas_call | solution.py:548
  14.3 0.8 %shard_map.105 = (f32[32,128]{1,0:T(8,128)}, f32[16,128]{1,0:T(8,128)}) custom-call(f32[16,128]{1,0:T(8,128)S(1)} %get-tuple-element.6.bounce_in, f32[16,128]{1,0:T(8,128)S(1)} %get-tuple-element.7.heat_ref, f32[1,128]{1,0:T(1,128)S(1)} %get-tuple-element.8.cond_ref, f32[32,128]{1,0:T(8,128)S(1)} %get-tuple-element.9.soil_ref), custom_call_target="tpu_custom_call" | custom-call | tf_op jit(solution)/shard_map/pallas_call | solution.py:571

commit v2 on v1

--- a/solution.py
+++ b/solution.py
@@ -16,6 +16,7 @@
 GROUP = 8
 CHUNK = 16
 TURNS = 32
+PAIR = 2
 
 
 def fourth(value):
@@ -262,11 +263,10 @@
     heat_ref,
     cond_ref,
     soil_ref,
-    alb_ref,
     tan_ref,
     occ_ref,
-    near,
-    far,
+    facts,
+    offsets,
     smp,
     planes,
     table,
@@ -281,15 +281,19 @@
     loads,
 ):
     n = n_recv * n_src
-    width = alb_ref.shape[1]
+    width = soil_ref.shape[1]
     n_samples = smp.shape[2]
     epochs = tan_ref.shape[1]
     bits = width.bit_length() - 1
-    rows = 2 * n
+    n_facts = facts.shape[0]
+    chip_bits = n_src.bit_length() - 1
+    quarter = n // 4
+    pitch = 2 * n + 8
     me = lax.axis_index("recv") * n_src + lax.axis_index("src")
+    chip = lax.axis_index("recv")
 
     def device(p):
-        return {"recv": p >> (n_src.bit_length() - 1), "src": p & (n_src - 1)}
+        return {"recv": p >> chip_bits, "src": p & (n_src - 1)}
 
     def greet(sem, p):
         pl.semaphore_signal(sem, inc=1, device_id=device(p), device_id_type=pl.DeviceIdType.MESH)
@@ -298,57 +302,60 @@
         lax.fori_loop(first, last, lambda p, c: (do(p), c)[1], 0)
 
     own = pl.ds(me, 1)
-    pairs = [(pos_in.at[pl.ds(c, 1)], near.at[c, own]) for c in range(3)]
-    pairs += [(smp_in, smp.at[me])]
-    pairs += [(nrm_in.at[pl.ds(c, 1)], far.at[c, own]) for c in range(3)]
-    pairs += [(area_in, far.at[3, own]), (alb_in, far.at[4, own]), (soil_in.at[pl.ds(0, 1)], far.at[5, own])]
-    pairs += [
-        (alb_in, alb_ref),
+    fill = [(pos_in.at[pl.ds(c, 1)], facts.at[c, own]) for c in range(3)]
+    fill += [(nrm_in.at[pl.ds(c, 1)], facts.at[3 + c, own]) for c in range(3)]
+    fill += [(area_in, facts.at[6, own]), (alb_in, facts.at[7, own])]
+    fill += [(soil_in.at[pl.ds(0, 1)], facts.at[8, own])]
+    for there, here in fill:
+        pltpu.make_async_copy(there, here, loads.at[0]).start()
+    pairs = (
+        (smp_in, offsets.at[me]),
         (tan_in, tan_ref),
         (soil_in, soil_ref),
         (cond_in, cond_ref),
         (occ_in.at[own], occ_ref),
-    ]
+    )
     fetched = [
-        pltpu.make_async_copy(there, here, loads.at[i]) for i, (there, here) in enumerate(pairs)
+        pltpu.make_async_copy(there, here, loads.at[1 + i]) for i, (there, here) in enumerate(pairs)
     ]
     for copy in fetched:
         copy.start()
     barrier = pltpu.get_barrier_semaphore()
     each(me + 1, n, lambda p: greet(barrier, p))
     pl.when(me > 0)(lambda: pl.semaphore_wait(barrier, me))
-    each(0, me, lambda p: greet(hello.at[me], p))
-
-    def parts(p, which):
-        ref = (near, smp, far)[which]
-        return ref.at[p] if which == 1 else ref.at[:, pl.ds(p, 1)]
-
-    def remote(slot, to, which):
+    each(0, me, lambda p: greet(hello.at[chip], p))
+
+    def remote(slots, to, sem):
         return pltpu.make_async_remote_copy(
-            src_ref=parts(slot, which),
-            dst_ref=parts(slot, which),
-            send_sem=sent.at[which],
-            recv_sem=got.at[which, slot],
+            src_ref=facts.at[:, slots],
+            dst_ref=facts.at[:, slots],
+            send_sem=sent.at[0],
+            recv_sem=got.at[sem],
             device_id=device(to),
             device_id_type=pl.DeviceIdType.MESH,
         )
 
-    for copy in fetched[:4]:
+    def remote_offsets(slot, to):
+        return pltpu.make_async_remote_copy(
+            src_ref=offsets.at[slot],
+            dst_ref=offsets.at[slot],
+            send_sem=sent.at[1],
+            recv_sem=got.at[n_recv],
+            device_id=device(to),
+            device_id_type=pl.DeviceIdType.MESH,
+        )
+
+    def tell(p):
+        remote(own, p, chip).start()
+        remote_offsets(me, p).start()
+
+    pltpu.make_async_copy(facts.at[:, own], facts.at[:, own], loads.at[0]).wait()
+    fetched[0].wait()
+    each(0, me, tell)
+    for copy in fetched[1:]:
         copy.wait()
 
-    def first(p):
-        remote(me, p, 0).start()
-        remote(me, p, 1).start()
-
-    each(0, me, first)
-    for copy in fetched[4:10]:
-        copy.wait()
-    each(0, me, lambda p: remote(me, p, 2).start())
-    for copy in fetched[10:]:
-        copy.wait()
-
-    mine = jnp.concatenate([near[:, me, :], far[0:3, me, :]], axis=0)
-    mine = jnp.concatenate([mine, mine[0:2]], axis=0)
+    mine = jnp.concatenate([facts[0:6, me, :], facts[0:2, me, :]], axis=0)
     tall = jnp.transpose(mine)
     for c in range(6):
         cols[c] = jnp.broadcast_to(tall[:, c : c + 1], (width, width))
@@ -365,19 +372,10 @@
     sun_ref[2] = jnp.broadcast_to(tan * cos_e, (epochs, width))
     sun_ref[3] = jnp.broadcast_to(tan, (epochs, width))
 
-    def answer(p):
-        pl.semaphore_wait(hello.at[p], 1)
-        remote(me, p, 0).start()
-        remote(me, p, 1).start()
-        remote(me, p, 2).start()
-
-    each(me + 1, n, answer)
-
     def see(p):
         weight = occ_ref[0, p].astype(jnp.float32)
         row = pl.ds(p, 1)
-        sx, sy, sz = (near[c, row, :] for c in range(3))
-        ox, oy, oz, size = (far[c, row, :] for c in range(4))
+        sx, sy, sz, ox, oy, oz, size = (facts[c, row, :] for c in range(7))
         scale = size * weight / math.pi
         for i in range(width // CHUNK):
             at = slice(i * CHUNK, (i + 1) * CHUNK)
@@ -390,45 +388,110 @@
             seen = jnp.maximum(facing, 0.0) * jnp.maximum(toward, 0.0) * scale
             view[p, at, :] = (seen / (spread * spread)).astype(jnp.bfloat16)
 
-    early = n - n // 8
+    see(me)
+    for other in range(1, n_src):
+        p = me ^ other
+
+        def answer_here():
+            pl.semaphore_wait(hello.at[chip], 1)
+            tell(p)
+
+        pl.when(p > me)(answer_here)
+
+    def answer(g):
+        pl.semaphore_wait(hello.at[g], n_src)
+        for core in range(n_src):
+            tell(g * n_src + core)
+
+    each(chip + 1, n_recv, answer)
+
+    for other in range(1, n_src):
+        remote(pl.ds(me ^ other, 1), me ^ other, chip).wait_recv()
+        see(me ^ other)
 
     def arrive(m):
-        p = me ^ m
-        for which in range(3):
-            remote(p, p, which).wait_recv()
-        see(p)
-
-    see(me)
-    each(1, early, arrive)
-    each(early, n, lambda m: [remote(me ^ m, me ^ m, which).wait_recv() for which in range(2)] and None)
-
+        g = chip ^ m
+        remote(pl.ds(g * n_src, n_src), me ^ 1, g).wait_recv()
+
+    def arrive_and_see(m):
+        arrive(m)
+        for core in range(n_src):
+            see((chip ^ m) * n_src + core)
+
+    late = n_recv - n_recv // 4
+    each(1, late, arrive_and_see)
+
+    def spread_rows():
+        for c in range(3):
+            planes[c, 0:8, :] = planes[c, n : n + 8, :]
+            planes[c, n + 8 : n + 16, :] = planes[c, 8:16, :]
+
+    def place(m):
+        start = ((me // quarter) ^ m) * quarter
+        for c in range(3):
+            planes[c, pl.ds(8 + start, quarter), :] = facts[c, pl.ds(start, quarter), :]
+
+    for m in range(3):
+        place(m)
+    gap = ((me // quarter) ^ 3) * quarter
     for c in range(3):
-        planes[c, 0:n, :] = near[c]
-        planes[c, n : n + 8, :] = near[c, 0:8]
+        planes[c, pl.ds(8 + gap, quarter), :] = jnp.zeros((quarter, width), jnp.float32)
+    spread_rows()
     lane = lax.broadcasted_iota(jnp.int32, (8, width), 1)
+
+    def turn(r, start, here, after):
+        mixed = jnp.where(lane >= r, here, after)
+        return pltpu.roll(mixed, (width - r) & (width - 1), 1)
 
     def spin(i, carry):
         for j in range(TURNS):
             r = i * TURNS + j
-            whole = lane >= r
-            back = (width - r) & (width - 1)
             for c in range(3):
                 for g in range(n // 8):
-                    here = planes[c, g * 8 : g * 8 + 8, :]
-                    after = planes[c, g * 8 + 1 : g * 8 + 9, :]
-                    turned = pltpu.roll(jnp.where(whole, here, after), back, 1)
-                    table[c, pl.ds(r * rows + g * 8, 8), :] = turned
-                    table[c, pl.ds(r * rows + n + g * 8, 8), :] = turned
+                    at = 8 + g * 8
+                    turned = turn(r, at, planes[c, at : at + 8, :], planes[c, at + 1 : at + 9, :])
+                    table[c, pl.ds(r * pitch + at, 8), :] = turned
+                    table[c, pl.ds(r * pitch + at + n, 8), :] = turned
         return carry
 
     lax.fori_loop(0, width // TURNS, spin, 0)
-
-    def horizons(a, carry):
-        here = [[planes[c, g * 8 : g * 8 + 8, :] for g in range(n // 8)] for c in range(3)]
+    each(late, n_recv, arrive)
+    remote_everything = pltpu.make_async_remote_copy(
+        src_ref=offsets.at[pl.ds(0, n - 1)],
+        dst_ref=offsets.at[pl.ds(0, n - 1)],
+        send_sem=sent.at[1],
+        recv_sem=got.at[n_recv],
+        device_id=device(me ^ 1),
+        device_id_type=pl.DeviceIdType.MESH,
+    )
+    remote_everything.wait_recv()
+    scalars = pltpu.make_async_copy(offsets, smp, loads.at[6])
+    scalars.start()
+    place(3)
+    spread_rows()
+
+    def respin(i, carry):
+        at = 7 + gap
+        for j in range(width // quarter):
+            r = i * (width // quarter) + j
+            for c in range(3):
+                here = planes[c, pl.ds(at, 8), :]
+                after = planes[c, pl.ds(at + 1, 8), :]
+                turned = turn(r, at, here, after)
+                table[c, pl.ds(r * pitch + at, 8), :] = turned
+                table[c, pl.ds(r * pitch + at + n, 8), :] = turned
+        see(gap + i)
+        return carry
+
+    lax.fori_loop(0, quarter, respin, 0)
+    scalars.wait()
+
+    def horizon(a):
+        here = [[planes[c, 8 + g * 8 : 16 + g * 8, :] for g in range(n // 8)] for c in range(3)]
         best = [jnp.full((8, width), -1e30, jnp.float32) for g in range(n // 8)]
         for s in range(n_samples):
             shift = smp[a, 0, s]
-            start = (shift & (width - 1)) * rows + (shift >> bits)
+            start = (shift & (width - 1)) * pitch + (shift >> bits) + 8
             for g in range(n // 8):
                 fx, fy, fz = (table[c, pl.ds(start + g * 8, 8), :] for c in range(3))
                 dx = fx - here[0][g]
@@ -440,19 +503,18 @@
         cx, cy, cz, tans = (sun_ref[c, line, :] for c in range(4))
         for g in range(n // 8):
             at = slice(g * 8, g * 8 + 8)
-            incidence = cx * far[0, at, :] + cy * far[1, at, :] + cz * far[2, at, :]
+            incidence = cx * facts[3, at, :] + cy * facts[4, at, :] + cz * facts[5, at, :]
             shade = jax.nn.sigmoid((tans - best[g]) / shade_width)
             direct = solar_flux * jnp.maximum(incidence, 0.0) * shade
             direct_ref[a, at, :] = direct
-            lit_ref[a, at, :] = far[4, at, :] * direct + emissivity * fourth(far[5, at, :])
+            lit_ref[a, at, :] = facts[7, at, :] * direct + emissivity * fourth(facts[8, at, :])
+
+    def horizons(i, carry):
+        for j in range(PAIR):
+            horizon(i * PAIR + j)
         return carry
 
-    def last(m):
-        remote(me ^ m, me ^ m, 2).wait_recv()
-        see(me ^ m)
-
-    each(early, n, last)
-    lax.fori_loop(0, epochs, horizons, 0)
+    lax.fori_loop(0, epochs // PAIR, horizons, 0)
 
     total = jnp.zeros((epochs, width), jnp.float32)
     for p in range(n):
@@ -463,9 +525,10 @@
             preferred_element_type=jnp.float32,
         )
     bounce_ref[...] = total
-    keep = surface_gain * (1.0 - alb_ref[...])
+    keep = surface_gain * (1.0 - facts[7, own, :])
     heat_ref[...] = keep * (direct_ref[:, me, :] + total)
-    each(1, n, lambda m: [remote(me, me, which).wait_send() for which in range(3)] and None)
+    remote(pl.ds(0, n - 1), me ^ 1, 0).wait_send()
+    remote_everything.wait_send()
 
 
 def conduct(bounce_in, heat_ref, cond_ref, soil_ref, final_ref, bounce_ref):
@@ -504,23 +567,22 @@
     if n <= 16:
         program = step
         scratch = [
-            pltpu.VMEM((1, width), f32),
             pltpu.VMEM((1, epochs), f32),
             pltpu.SMEM((1, occupancy.shape[1]), jnp.int32),
-            pltpu.VMEM((3, n, width), f32),
-            pltpu.VMEM((6, n, width), f32),
+            pltpu.VMEM((9, n, width), f32),
+            pltpu.VMEM((n, 1, n_samples), jnp.int32),
             pltpu.SMEM((n, 1, n_samples), jnp.int32),
-            pltpu.VMEM((3, n + 8, width), f32),
-            pltpu.VMEM((3, width * 2 * n, width), f32),
+            pltpu.VMEM((3, n + 16, width), f32),
+            pltpu.VMEM((3, width * (2 * n + 8) + 8, width), f32),
             pltpu.VMEM((6, width, width), f32),
             pltpu.VMEM((n, width, width), jnp.bfloat16),
             pltpu.VMEM((4, epochs, width), f32),
             pltpu.VMEM((epochs, n, width), f32),
             pltpu.VMEM((epochs, n, width), f32),
-            pltpu.SemaphoreType.REGULAR((n,)),
-            pltpu.SemaphoreType.DMA((3,)),
-            pltpu.SemaphoreType.DMA((3, n)),
-            pltpu.SemaphoreType.DMA((15,)),
+            pltpu.SemaphoreType.REGULAR((n_recv,)),
+            pltpu.SemaphoreType.DMA((2,)),
+            pltpu.SemaphoreType.DMA((n_recv + 1,)),
+            pltpu.SemaphoreType.DMA((7,)),
         ]
     else:
         program = kernel

time: 15.3 us -> 14 us (0.915)
  Pallas kernels: 14.5 us -> 13.2 us
    pallas_call x1, Pallas kernels: 13.6 us -> 12.4 us  [body(): pl.pallas_call(functools.partial(program, n_recv, n_src), out_shape=(pltp...]
where the time goes in v2:
time: 14 us; the launch traced here: 13.9 us
  Pallas kernels  13.2 us (94%)
  between operations  0.64 us (5%)
    pallas_call x1, Pallas kernels, body(): pl.pallas_call(functools.partial(program, n_recv, n_src), out_shape=(pltp...  12.4 us
    pallas_call x1, Pallas kernels, body(): pl.pallas_call(conduct, out_shape=(jax.ShapeDtypeStruct(soil.shape, f32),...  0.81 us

profile of v2, /device:TPU:0, one launch (start us, length us, event | category | flops | bytes accessed | tf_op | source)
XLA Modules:
  0.0 13.9 jit_solution(9836730647903025711)
XLA Ops:
  0.6 12.4 %shard_map.104 = (f32[16,128]{1,0:T(8,128)S(1)}, f32[16,128]{1,0:T(8,128)S(1)}, f32[1,128]{1,0:T(1,128)S(1)}, f32[32,128]{1,0:T(8,128)S(1)}) custom-call(f32[3,128]{1,0:T(4,128)} %pos_in.1, f32[3,128]{1,0:T(4,128)} %nrm_in.1, f32[1,128]{1,0:T(1,128)} %bitcast.4, f32[1,128]{1,0:T(1,128)} %bitcast.5, f32[1,128]{1,0:T(1,128)} %bitcast.6, f32[32,128]{1,0:T(8,128)} %soil_in.1, ...), custom_call_target="tpu_custom_call" | custom-call | tf_op jit(solution)/shard_map/pallas_call | solution.py:610
  13.1 0.8 %shard_map.105 = (f32[32,128]{1,0:T(8,128)}, f32[16,128]{1,0:T(8,128)}) custom-call(f32[16,128]{1,0:T(8,128)S(1)} %get-tuple-element.6.bounce_in, f32[16,128]{1,0:T(8,128)S(1)} %get-tuple-element.7.heat_ref, f32[1,128]{1,0:T(1,128)S(1)} %get-tuple-element.8.cond_ref, f32[32,128]{1,0:T(8,128)S(1)} %get-tuple-element.9.soil_ref), custom_call_target="tpu_custom_call" | custom-call | tf_op jit(solution)/shard_map/pallas_call | solution.py:633

commit v3 on v2

--- a/solution.py
+++ b/solution.py
@@ -16,7 +16,8 @@
 GROUP = 8
 CHUNK = 16
 TURNS = 32
-PAIR = 2
+PATCH = 64
+PAIR = 4
 
 
 def fourth(value):
@@ -340,7 +341,7 @@
             src_ref=offsets.at[slot],
             dst_ref=offsets.at[slot],
             send_sem=sent.at[1],
-            recv_sem=got.at[n_recv],
+            recv_sem=got.at[n_recv + slot // quarter],
             device_id=device(to),
             device_id_type=pl.DeviceIdType.MESH,
         )
@@ -372,12 +373,13 @@
     sun_ref[2] = jnp.broadcast_to(tan * cos_e, (epochs, width))
     sun_ref[3] = jnp.broadcast_to(tan, (epochs, width))
 
-    def see(p):
+    def glimpses(p):
         weight = occ_ref[0, p].astype(jnp.float32)
         row = pl.ds(p, 1)
         sx, sy, sz, ox, oy, oz, size = (facts[c, row, :] for c in range(7))
         scale = size * weight / math.pi
-        for i in range(width // CHUNK):
+
+        def glimpse(i):
             at = slice(i * CHUNK, (i + 1) * CHUNK)
             dx = sx - cols[0, at, :]
             dy = sy - cols[1, at, :]
@@ -388,6 +390,12 @@
             seen = jnp.maximum(facing, 0.0) * jnp.maximum(toward, 0.0) * scale
             view[p, at, :] = (seen / (spread * spread)).astype(jnp.bfloat16)
 
+        return [functools.partial(glimpse, i) for i in range(width // CHUNK)]
+
+    def see(p):
+        for glimpse in glimpses(p):
+            glimpse()
+
     see(me)
     for other in range(1, n_src):
         p = me ^ other
@@ -439,7 +447,7 @@
     spread_rows()
     lane = lax.broadcasted_iota(jnp.int32, (8, width), 1)
 
-    def turn(r, start, here, after):
+    def turn(r, here, after):
         mixed = jnp.where(lane >= r, here, after)
         return pltpu.roll(mixed, (width - r) & (width - 1), 1)
 
@@ -449,42 +457,55 @@
             for c in range(3):
                 for g in range(n // 8):
                     at = 8 + g * 8
-                    turned = turn(r, at, planes[c, at : at + 8, :], planes[c, at + 1 : at + 9, :])
+                    turned = turn(r, planes[c, at : at + 8, :], planes[c, at + 1 : at + 9, :])
                     table[c, pl.ds(r * pitch + at, 8), :] = turned
                     table[c, pl.ds(r * pitch + at + n, 8), :] = turned
         return carry
 
+    def samples_of(m, count):
+        slots = pl.ds(0, count)
+        return pltpu.make_async_remote_copy(
+            src_ref=offsets.at[slots],
+            dst_ref=offsets.at[slots],
+            send_sem=sent.at[1],
+            recv_sem=got.at[n_recv + ((me // quarter) ^ m)],
+            device_id=device(me ^ 1),
+            device_id_type=pl.DeviceIdType.MESH,
+        )
+
+    def to_scalars(m):
+        slots = pl.ds(((me // quarter) ^ m) * quarter, quarter)
+        return pltpu.make_async_copy(offsets.at[slots], smp.at[slots], loads.at[6 + m])
+
+    for m in range(3):
+        samples_of(m, quarter - (m == 0)).wait_recv()
+        to_scalars(m).start()
     lax.fori_loop(0, width // TURNS, spin, 0)
     each(late, n_recv, arrive)
-    remote_everything = pltpu.make_async_remote_copy(
-        src_ref=offsets.at[pl.ds(0, n - 1)],
-        dst_ref=offsets.at[pl.ds(0, n - 1)],
-        send_sem=sent.at[1],
-        recv_sem=got.at[n_recv],
-        device_id=device(me ^ 1),
-        device_id_type=pl.DeviceIdType.MESH,
-    )
-    remote_everything.wait_recv()
-    scalars = pltpu.make_async_copy(offsets, smp, loads.at[6])
-    scalars.start()
+    samples_of(3, quarter).wait_recv()
+    to_scalars(3).start()
     place(3)
     spread_rows()
 
+    at = 7 + gap
+    window = [[planes[c, pl.ds(at + k, 8), :] for k in range(2)] for c in range(3)]
+
     def respin(i, carry):
-        at = 7 + gap
-        for j in range(width // quarter):
-            r = i * (width // quarter) + j
+        blocks = quarter * PATCH // width
+        todo = [g for j in range(blocks) for g in glimpses(gap + i * blocks + j)]
+        for j in range(PATCH):
+            r = i * PATCH + j
             for c in range(3):
-                here = planes[c, pl.ds(at, 8), :]
-                after = planes[c, pl.ds(at + 1, 8), :]
-                turned = turn(r, at, here, after)
+                turned = turn(r, window[c][0], window[c][1])
                 table[c, pl.ds(r * pitch + at, 8), :] = turned
                 table[c, pl.ds(r * pitch + at + n, 8), :] = turned
-        see(gap + i)
+            if j % (PATCH // len(todo)) == 0:
+                todo[j // (PATCH // len(todo))]()
         return carry
 
-    lax.fori_loop(0, quarter, respin, 0)
-    scalars.wait()
+    lax.fori_loop(0, width // PATCH, respin, 0)
+    for m in range(3):
+        to_scalars(m).wait()
 
     def horizon(a):
         here = [[planes[c, 8 + g * 8 : 16 + g * 8, :] for g in range(n // 8)] for c in range(3)]
@@ -496,8 +517,7 @@
                 fx, fy, fz = (table[c, pl.ds(start + g * 8, 8), :] for c in range(3))
                 dx = fx - here[0][g]
                 dy = fy - here[1][g]
-                square = jnp.maximum(dx * dx + dy * dy, 1e-30)
-                reach = square * lax.rsqrt(square) + reach_offset
+                reach = 1.0 / lax.rsqrt(dx * dx + dy * dy) + reach_offset
                 best[g] = jnp.maximum(best[g], (fz - here[2][g]) / reach)
         line = pl.ds(a, 1)
         cx, cy, cz, tans = (sun_ref[c, line, :] for c in range(4))
@@ -506,29 +526,68 @@
             incidence = cx * facts[3, at, :] + cy * facts[4, at, :] + cz * facts[5, at, :]
             shade = jax.nn.sigmoid((tans - best[g]) / shade_width)
             direct = solar_flux * jnp.maximum(incidence, 0.0) * shade
-            direct_ref[a, at, :] = direct
-            lit_ref[a, at, :] = facts[7, at, :] * direct + emissivity * fourth(facts[8, at, :])
+            put = pl.ds(pl.multiple_of(a * n + g * 8, 8), 8)
+            direct_ref[put, :] = direct
+            lit_ref[put, :] = facts[7, at, :] * direct + emissivity * fourth(facts[8, at, :])
+
+    shared = epochs // 4
+    core = me & 1
+    partner = me ^ 1
+
+    def azimuth(order):
+        return ((me // quarter) ^ (order // quarter)) * quarter + (order & (quarter - 1))
+
+    def swap(ref, which):
+        return pltpu.make_async_remote_copy(
+            src_ref=ref,
+            dst_ref=ref,
+            send_sem=sent.at[2 + which],
+            recv_sem=got.at[n_recv + 4 + which],
+            device_id=device(partner),
+            device_id_type=pl.DeviceIdType.MESH,
+        )
+
+    def swaps(first, facet):
+        start = pl.multiple_of(azimuth(first) * n, 8)
+        lines = [direct_ref.at[pl.ds(start + k * n + facet, 1)] for k in range(shared)]
+        return [swap(lit_ref.at[pl.ds(start, shared * n)], 0)] + [swap(line, 1) for line in lines]
+
+    swapped = (swap(lit_ref.at[pl.ds(0, shared * n)], 0), swap(direct_ref.at[pl.ds(0, shared)], 1))
 
     def horizons(i, carry):
+        @pl.when(i == shared // PAIR)
+        def _():
+            for copy in swaps(core * shared, partner):
+                copy.start()
+
+        @pl.when(i == 2 * shared // PAIR)
+        def _():
+            to_scalars(3).wait()
+
+        first = jnp.where(i < shared // PAIR, core * shared, shared) + i * PAIR
         for j in range(PAIR):
-            horizon(i * PAIR + j)
+            horizon(azimuth(first + j))
         return carry
 
-    lax.fori_loop(0, epochs // PAIR, horizons, 0)
+    lax.fori_loop(0, 3 * shared // PAIR, horizons, 0)
+    for copy in swapped:
+        copy.wait_recv()
 
     total = jnp.zeros((epochs, width), jnp.float32)
     for p in range(n):
         total = total + lax.dot_general(
-            lit_ref[:, p, :].astype(jnp.bfloat16),
+            lit_ref[pl.ds(p, epochs, stride=n), :].astype(jnp.bfloat16),
             view[p],
             (((1,), (1,)), ((), ())),
             preferred_element_type=jnp.float32,
         )
     bounce_ref[...] = total
     keep = surface_gain * (1.0 - facts[7, own, :])
-    heat_ref[...] = keep * (direct_ref[:, me, :] + total)
+    heat_ref[...] = keep * (direct_ref[pl.ds(me, epochs, stride=n), :] + total)
     remote(pl.ds(0, n - 1), me ^ 1, 0).wait_send()
-    remote_everything.wait_send()
+    samples_of(0, n - 1).wait_send()
+    for copy in swapped:
+        copy.wait_send()
 
 
 def conduct(bounce_in, heat_ref, cond_ref, soil_ref, final_ref, bounce_ref):
@@ -577,12 +636,12 @@
             pltpu.VMEM((6, width, width), f32),
             pltpu.VMEM((n, width, width), jnp.bfloat16),
             pltpu.VMEM((4, epochs, width), f32),
-            pltpu.VMEM((epochs, n, width), f32),
-            pltpu.VMEM((epochs, n, width), f32),
+            pltpu.VMEM((epochs * n, width), f32),
+            pltpu.VMEM((epochs * n, width), f32),
             pltpu.SemaphoreType.REGULAR((n_recv,)),
-            pltpu.SemaphoreType.DMA((2,)),
-            pltpu.SemaphoreType.DMA((n_recv + 1,)),
-            pltpu.SemaphoreType.DMA((7,)),
+            pltpu.SemaphoreType.DMA((4,)),
+            pltpu.SemaphoreType.DMA((n_recv + 6,)),
+            pltpu.SemaphoreType.DMA((10,)),
         ]
     else:
         program = kernel

time: 14 us -> 13.4 us (0.957)
  Pallas kernels: 13.2 us -> 12.6 us
    pallas_call x1, Pallas kernels: 12.4 us -> 11.8 us  [body(): pl.pallas_call(functools.partial(program, n_recv, n_src), out_shape=(pltp...]
where the time goes in v3:
time: 13.4 us; the launch traced here: 13.2 us
  Pallas kernels  12.6 us (94%)
  between operations  0.64 us (5%)
    pallas_call x1, Pallas kernels, body(): pl.pallas_call(functools.partial(program, n_recv, n_src), out_shape=(pltp...  11.8 us
    pallas_call x1, Pallas kernels, body(): pl.pallas_call(conduct, out_shape=(jax.ShapeDtypeStruct(soil.shape, f32),...  0.81 us

profile of v3, /device:TPU:0, one launch (start us, length us, event | category | flops | bytes accessed | tf_op | source)
XLA Modules:
  0.0 13.2 jit_solution(14979839316062005975)
XLA Ops:
  0.6 11.8 %shard_map.104 = (f32[16,128]{1,0:T(8,128)S(1)}, f32[16,128]{1,0:T(8,128)S(1)}, f32[1,128]{1,0:T(1,128)S(1)}, f32[32,128]{1,0:T(8,128)S(1)}) custom-call(f32[3,128]{1,0:T(4,128)} %pos_in.1, f32[3,128]{1,0:T(4,128)} %nrm_in.1, f32[1,128]{1,0:T(1,128)} %bitcast.4, f32[1,128]{1,0:T(1,128)} %bitcast.5, f32[1,128]{1,0:T(1,128)} %bitcast.6, f32[32,128]{1,0:T(8,128)} %soil_in.1, ...), custom_call_target="tpu_custom_call" | custom-call | tf_op jit(solution)/shard_map/pallas_call | solution.py:669
  12.4 0.8 %shard_map.105 = (f32[32,128]{1,0:T(8,128)}, f32[16,128]{1,0:T(8,128)}) custom-call(f32[16,128]{1,0:T(8,128)S(1)} %get-tuple-element.6.bounce_in, f32[16,128]{1,0:T(8,128)S(1)} %get-tuple-element.7.heat_ref, f32[1,128]{1,0:T(1,128)S(1)} %get-tuple-element.8.cond_ref, f32[32,128]{1,0:T(8,128)S(1)} %get-tuple-element.9.soil_ref), custom_call_target="tpu_custom_call" | custom-call | tf_op jit(solution)/shard_map/pallas_call | solution.py:692
